TPU v7x, 32 devices: a 4x4x1 block of a 4x4x8 slice. The times are simulated.
32 devices in a mesh: dp: 2 (over z, core), ep: 16 (over x, y).
Axes of the slice: x: 4, y: 4, z: 1, core: 2. Of those that a mesh axis runs over, the one named last changes fastest.
The devices are a block of a 4x4x8 slice.
Arguments:
- x: bfloat16 [2, 16, 256, 2560], P('dp', 'ep'), parts along dimension 0
- expert: int32 [2, 16, 256, 8], P('dp', 'ep'), parts along dimension 0
- slot: int32 [2, 16, 256, 8], P('dp', 'ep'), parts along dimension 0
- gate: float32 [2, 16, 256, 8], P('dp', 'ep'), parts along dimension 0
- w_gate: bfloat16 [80, 2560, 1536], P('ep')
- w_up: bfloat16 [80, 2560, 1536], P('ep')
- w_down: bfloat16 [80, 1536, 2560], P('ep')
- s_gate: bfloat16 [2560, 1536], replicated
- s_up: bfloat16 [2560, 1536], replicated
- s_down: bfloat16 [1536, 2560], replicated
Outputs:
- y: bfloat16 [2, 16, 256, 2560], P('dp', 'ep'), parts along dimension 0
There are 2 independent parts. A program takes and returns all parts, laid end to end along the dimension named above; an argument that names none is the same for every part.
All inputs are finite; a program needn't handle non-finite values.
Results may differ from a plain program's by a relative error of at most 0.009.
Values are sent between devices in bfloat16 or wider.
A program may use at most 768 MiB of HBM per device.

v0:
```python
import jax
import jax.numpy as jnp
from jax import lax
from jax.sharding import NamedSharding, PartitionSpec as P


def einsum(form, a, b):
    return jnp.einsum(form, a.astype(jnp.float32), b.astype(jnp.float32))


def for_all(x, s_gate, s_up, s_down):
    h = jax.nn.silu(einsum("...d,df->...f", x, s_gate)) * einsum("...d,df->...f", x, s_up)
    return einsum("...f,fd->...d", h.astype(jnp.bfloat16), s_down)


def solution(mesh):
    def placed(v, *spec):
        return lax.with_sharding_constraint(v, NamedSharding(mesh, P(*spec)))

    def step(x, expert, slot, gate, w_gate, w_up, w_down, s_gate, s_up, s_down):
        experts, (tokens, top) = w_gate.shape[0], expert.shape[2:]
        slots = 5 * tokens * top // (4 * experts)
        to_expert = jax.nn.one_hot(expert, experts, dtype=jnp.bfloat16)
        to_slot = jax.nn.one_hot(slot, slots, dtype=jnp.bfloat16)
        weighted = to_expert * gate[..., None].astype(jnp.bfloat16)
        dispatch = einsum("abtke,abtkc->abtec", to_expert, to_slot).astype(jnp.bfloat16)
        combine = einsum("abtke,abtkc->abtec", weighted, to_slot).astype(jnp.bfloat16)
        z = einsum("abtec,abtd->aebcd", dispatch, x).astype(jnp.bfloat16)
        z = placed(z, "dp", None, "ep", None, None)
        z = placed(z, "dp", "ep", None, None, None)
        h = jax.nn.silu(einsum("aebcd,edf->aebcf", z, w_gate))
        h = (h * einsum("aebcd,edf->aebcf", z, w_up)).astype(jnp.bfloat16)
        out = einsum("aebcf,efd->aebcd", h, w_down).astype(jnp.bfloat16)
        out = placed(out, "dp", "ep", None, None, None)
        out = placed(out, "dp", None, "ep", None, None)
        y = einsum("abtec,aebcd->abtd", combine, out)
        return (y + for_all(x, s_gate, s_up, s_down)).astype(jnp.bfloat16)

    return step
```

profile of v0, /device:TPU:96, one launch (start us, length us, event | category | flops | bytes accessed | tf_op | source)
XLA Modules:
  0.0 517.4 jit_solution(16742588098160739173)
XLA Ops:
  0.0 0.0 copy-start
  0.0 0.9 copy.10
  0.9 0.0 copy-start.1
  0.9 1.5 copy.12
  2.5 3.6 convolution_convert_fusion.2
  6.1 3.0 copy.13
  9.1 0.0 copy-done
  9.1 5.1 convolution_convert_fusion
  14.2 0.0 copy-done.1
  14.2 168.8 %all-to-all.4 = bf16[1,16,5,1,32,2560]{5,4,2,3,0,1:T(8,128)(2,1)} all-to-all(bf16[1,16,5,1,32,2560]{5,4,2,3,0,1:T(8,128)(2,1)S(1)} %bitcast.117), channel_id=1, replica_groups=mesh['dp'=2,'ep'=16] {'ep'}, dimensions={1} | all-to-all | bytes 26214400 | tf_op jit(solution)/sharding_constraint;jit(solution)/sharding_constraint | solution.py:18
  183.0 30.1 %fusion.2 = f32[5,16,32,1536]{3,2,1,0:T(8,128)} fusion(bf16[5,2560,1536]{2,1,0:T(8,128)(2,1)} %param.5, bf16[1,16,5,1,32,2560]{5,4,2,3,0,1:T(8,128)(2,1)} %all-to-all.4), kind=kOutput, calls=%fused_computation.2 | convolution fusion | flops 20132659200 | bytes 68157440 | tf_op jit(solution)/aebcd,edf->aebcf/dot_general | solution.py:8
  213.1 30.2 %fusion.4 = f32[5,16,32,1536]{3,2,1,0:T(8,128)} fusion(bf16[5,2560,1536]{2,1,0:T(8,128)(2,1)} %param.4, bf16[1,16,5,1,32,2560]{5,4,2,3,0,1:T(8,128)(2,1)} %all-to-all.4), kind=kOutput, calls=%fused_computation.4 | convolution fusion | flops 20132659200 | bytes 68157440 | tf_op jit(solution)/aebcd,edf->aebcf/dot_general | solution.py:8
  243.3 28.2 %convert_bitcast_fusion = bf16[1,5,16,1,32,2560]{5,4,2,1,3,0:T(8,128)(2,1)S(1)} fusion(bf16[5,1536,2560]{2,1,0:T(8,128)(2,1)} %param.6, f32[5,16,32,1536]{3,2,1,0:T(8,128)} %fusion.2, f32[5,16,32,1536]{3,2,1,0:T(8,128)} %fusion.4), kind=kOutput, calls=%fused_computation.15 | convolution fusion | flops 20162805760 | bytes 83886080 | tf_op jit(solution)/aebcf,efd->aebcd/dot_general | solution.py:8
  271.5 6.5 %copy.16 = bf16[1,5,16,1,32,2560]{5,4,1,3,0,2:T(8,128)(2,1)} copy(bf16[1,5,16,1,32,2560]{5,4,2,1,3,0:T(8,128)(2,1)S(1)} %convert_bitcast_fusion) | data formatting | bytes 26214400 | tf_op jit(solution)/sharding_constraint;jit(solution)/sharding_constraint | solution.py:18
  278.0 0.0 copy-start.4
  278.0 0.0 copy-start.2
  278.0 0.0 copy-start.3
  278.0 5.7 %all-to-all-start.1 = ((bf16[1,5,16,1,32,2560]{5,4,1,3,0,2:T(8,128)(2,1)}), bf16[1,5,16,1,32,2560]{5,4,1,3,0,2:T(8,128)(2,1)}, u32[]{:S(2)}, u32[]{:S(2)}) async-start(bf16[1,5,16,1,32,2560]{5,4,1,3,0,2:T(8,128)(2,1)} %copy.16), calls=%async_computation.1 | async-start | bytes 26214400 | tf_op jit(solution)/sharding_constraint;jit(solution)/sharding_constraint | solution.py:18
  283.7 0.0 copy-done.4
  283.8 0.1 copy.11
  283.9 0.0 copy-done.2
  283.9 0.0 copy-done.3
  283.9 4.0 convolution_convert_fusion.1
  287.9 3.6 copy.23
  291.5 6.6 %convolution_bitcast_fusion.2 = f32[1,1,256,1536]{3,2,1,0:T(8,128)} fusion(bf16[2560,1536]{1,0:T(8,128)(2,1)} %param.7, bf16[1,1,256,2560]{3,2,1,0:T(8,128)(2,1)S(1)} %copy-done), kind=kOutput, calls=%fused_computation.26 | convolution fusion | flops 2013265920 | bytes 10747904 | tf_op jit(solution)/...d,df->...f/dot_general | solution.py:8
  298.2 11.7 %fusion.34 = f32[256,2560]{1,0:T(8,128)} fusion(bf16[1536,2560]{1,0:T(8,128)(2,1)} %param.9, bf16[2560,1536]{1,0:T(8,128)(2,1)} %param.8, f32[1,1,256,1536]{3,2,1,0:T(8,128)} %convolution_bitcast_fusion.2, bf16[1,1,256,2560]{3,2,1,0:T(8,128)(2,1)S(1)} %copy-done), kind=kOutput, calls=%fused_computation.39 | convolution fusion | flops 4028891136 | bytes 21233664 | tf_op jit(solution)/...f,fd->...d/dot_general | solution.py:8
  309.8 197.7 %all-to-all-done.1 = bf16[1,5,16,1,32,2560]{5,4,1,3,0,2:T(8,128)(2,1)} async-done(((bf16[1,5,16,1,32,2560]{5,4,1,3,0,2:T(8,128)(2,1)}), bf16[1,5,16,1,32,2560]{5,4,1,3,0,2:T(8,128)(2,1)}, u32[]{:S(2)}, u32[]{:S(2)}) %all-to-all-start.1) | async-done | bytes 13107232 | tf_op jit(solution)/sharding_constraint;jit(solution)/sharding_constraint | solution.py:18
  507.6 9.8 %fusion.20 = bf16[1,1,256,2560]{3,2,1,0:T(8,128)(2,1)} fusion(f32[256,2560]{1,0:T(8,128)} %fusion.34, bf16[256,80,32]{0,2,1:T(8,128)(2,1)S(1)} %copy.23, bf16[80,32,2560]{2,1,0:T(8,128)(2,1)} %bitcast.25), kind=kOutput, calls=%fused_computation.23 | convolution fusion | flops 3356753920 | bytes 18350080 | tf_op jit(solution)/abtec,aebcd->abtd/dot_general | solution.py:8
  (1 shorter events, 0.0 us)
Async XLA Ops:
  0.0 9.1 %copy-start = (bf16[1,1,256,2560]{3,2,1,0:T(8,128)(2,1)S(1)}, bf16[1,1,256,2560]{3,2,1,0:T(8,128)(2,1)}, u32[]{:S(2)}) copy-start(bf16[1,1,256,2560]{3,2,1,0:T(8,128)(2,1)} %param.3) | copy-start | bytes 3932164
  0.9 13.3 %copy-start.1 = (s32[256,8]{1,0:T(8,128)}, s32[256,8]{1,0:T(8,128)S(1)}, u32[]{:S(2)}) copy-start(s32[256,8]{1,0:T(8,128)S(1)} %copy.10) | copy-start | bytes 24580
  278.0 5.7 %copy-start.4 = (f32[1,1,256,8]{2,3,1,0:T(8,128)S(1)}, f32[1,1,256,8]{2,3,1,0:T(8,128)}, u32[]{:S(2)}) copy-start(f32[1,1,256,8]{2,3,1,0:T(8,128)} %param.1) | copy-start | bytes 24580
  278.0 5.9 %copy-start.2 = (s32[256,8]{1,0:T(8,128)S(1)}, s32[256,8]{1,0:T(8,128)}, u32[]{:S(2)}) copy-start(s32[256,8]{1,0:T(8,128)} %copy-done.1) | copy-start | bytes 24580
  278.0 5.9 %copy-start.3 = (s32[256,8]{1,0:T(8,128)S(1)}, s32[256,8]{1,0:T(8,128)}, u32[]{:S(2)}) copy-start(s32[256,8]{1,0:T(8,128)} %copy.12) | copy-start | bytes 24580
  278.0 229.6 %all-to-all-start.1 = ((bf16[1,5,16,1,32,2560]{5,4,1,3,0,2:T(8,128)(2,1)}), bf16[1,5,16,1,32,2560]{5,4,1,3,0,2:T(8,128)(2,1)}, u32[]{:S(2)}, u32[]{:S(2)}) async-start(bf16[1,5,16,1,32,2560]{5,4,1,3,0,2:T(8,128)(2,1)} %copy.16), calls=%async_computation.1 | async-start | bytes 26214400 | tf_op jit(solution)/sharding_constraint;jit(solution)/sharding_constraint | solution.py:18
where the time goes:
time: 518 us; the launch traced here: 517 us
  waiting for transfers between devices  198 us (38%)
  blocking collectives  169 us (33%)
  matrix products  129 us (25%)
  local copies, waits for them, and re-layouts  15.7 us (3%)
  starting transfers between devices  5.71 us (1%)
    another operation x1, waiting for transfers between devices, placed(): return lax.with_sharding_constraint(v, NamedSharding(mesh, P(*spec)))  198 us
    another operation x1, blocking collectives, placed(): return lax.with_sharding_constraint(v, NamedSharding(mesh, P(*spec)))  169 us
    dot_general x9, matrix products, einsum(): return jnp.einsum(form, a.astype(jnp.float32), b.astype(jnp.float32))  129 us
  transfers between devices with their start and end apart: 1, of which 1 were waited for; matrix products, arithmetic and copies ran while one was open for 5% of the time, Pallas kernels for 0%

commit v1 on v0

v1 whole, which is shorter than its diff:
```python
import functools
import math

import jax
import jax.numpy as jnp
from jax import lax
from jax.experimental import pallas as pl
from jax.experimental.pallas import tpu as pltpu
from jax.sharding import PartitionSpec as P

MESH = pl.DeviceIdType.MESH
F32, BF16 = jnp.float32, jnp.bfloat16
VMEM_BYTES = 67_000_000
HALF = 256


def dot(a, b):
    return jnp.dot(a, b, preferred_element_type=F32)


class Place:
    def __init__(self, side):
        me = lax.axis_index("ep")
        self.side, self.x, self.y = side, me // side, me % side

    def at(self, dx, dy):
        s = self.side
        return (self.x + (dx % s)) % s * s + (self.y + (dy % s)) % s

    def first(self, half, d):
        return self.at(d, 0) if half == 0 else self.at(0, d)

    def second(self, half, d):
        return self.at(0, d) if half == 0 else self.at(d, 0)


def hits(rt, base, rows, tokens, weighted):
    row = lax.broadcasted_iota(jnp.int32, (rows, tokens), 0).astype(F32) + base.astype(F32)
    top = rt.shape[0] // 2
    total = jnp.zeros((rows, tokens), F32)
    for k in range(top):
        value = rt[top + k : top + k + 1, :] if weighted else jnp.ones((1, tokens), F32)
        total = total + jnp.where(rt[k : k + 1, :] == row, value, 0.0)
    return total


def expert_in(side, slots, chunks, rt_ref, x_ref, wg_hbm, wu_hbm, h_hbm, rt_out,
              rtb, raw, tran, pk, zb, dm, wgb, wub, accg, accu, ze, hst,
              rs, rr, ps, pr, ws, hs):
    place = Place(side)
    tokens, rows = x_ref.shape[0], dm.shape[3]
    experts, _, ff = accg.shape
    wide = 2 * HALF
    part = wgb.shape[2]
    parts = ff // part
    steps = chunks * experts * parts
    hops = range(1, side)

    barrier = pltpu.get_barrier_semaphore()
    for half in (0, 1):
        for d in hops:
            pl.semaphore_signal(barrier, inc=1, device_id={"ep": place.first(half, d)}, device_id_type=MESH)

    def weights(step):
        slot = step % 3
        c, e, n = step // (experts * parts), step // parts % experts, step % parts
        at = (e, pl.ds(pl.multiple_of(c * wide, wide), wide), pl.ds(pl.multiple_of(n * part, part), part))
        return (
            pltpu.make_async_copy(wg_hbm.at[at], wgb.at[slot], ws.at[0, slot]),
            pltpu.make_async_copy(wu_hbm.at[at], wub.at[slot], ws.at[1, slot]),
        )

    for step in (0, 1):
        for copy in weights(step):
            copy.start()
    for half in (0, 1):
        rtb[half, 0] = rt_ref[...]
    pl.semaphore_wait(barrier, 2 * (side - 1))

    def routing(half, d):
        return pltpu.make_async_remote_copy(
            src_ref=rt_ref, dst_ref=rtb.at[half, side - d], send_sem=rs.at[half, d], recv_sem=rr.at[half, side - d],
            device_id={"ep": place.first(half, d)}, device_id_type=MESH)

    def cols(half, c):
        return pl.ds(pl.multiple_of(c * wide + half * HALF, HALF), HALF)

    low, high = pl.ds(0, tokens // 2), pl.ds(tokens // 2, tokens // 2)

    def send(kind, half, c):
        plus, minus = (1, -1)
        src, dst, to = [
            lambda: (x_ref.at[:, cols(half, c)], raw.at[half, c, 2], place.first(half, plus)),
            lambda: (x_ref.at[:, cols(half, c)], raw.at[half, c, 0], place.first(half, minus)),
            lambda: (raw.at[half, c, 2, low], raw.at[half, c, 1, low], place.first(half, plus)),
            lambda: (raw.at[half, c, 0, high], raw.at[half, c, 1, high], place.first(half, minus)),
            lambda: (pk.at[half, 1, pl.ds(0, 2)], tran.at[half, c, 0], place.second(half, plus)),
            lambda: (pk.at[half, 1, pl.ds(2, 2)], tran.at[half, c, 1], place.second(half, minus)),
            lambda: (pk.at[half, 0], zb.at[half, c, 3], place.second(half, plus)),
            lambda: (pk.at[half, 2], zb.at[half, c, 1], place.second(half, minus)),
            lambda: (tran.at[half, c, 0], zb.at[half, c, 2, pl.ds(0, 2)], place.second(half, plus)),
            lambda: (tran.at[half, c, 1], zb.at[half, c, 2, pl.ds(2, 2)], place.second(half, minus)),
        ][kind]()
        return pltpu.make_async_remote_copy(
            src_ref=src, dst_ref=dst, send_sem=ps.at[kind, half, c], recv_sem=pr.at[kind, half, c],
            device_id={"ep": to}, device_id_type=MESH)

    def own_blocks(c):
        for half in (0, 1):
            send(0, half, c).start()
            send(1, half, c).start()

    def pass_blocks(c):
        for half in (0, 1):
            send(0, half, c).wait_recv()
            send(2, half, c).start()
            send(1, half, c).wait_recv()
            send(3, half, c).start()

    def pick(half, c, j):
        for r in range(side):
            block = x_ref[:, cols(half, c)] if r == 0 else raw[half, c, r - 1]
            rows_out = dot(dm[half, j, r], block).astype(BF16)
            if j == 0:
                zb[half, c, 0, r] = rows_out
            else:
                pk[half, j - 1, r] = rows_out

    def relay(c):
        for half in (0, 1):

            @pl.when(c > 0)
            def _():
                for kind in (4, 5, 6, 7):
                    send(kind, half, c - 1).wait_send()

            send(2, half, c).wait_recv()
            send(3, half, c).wait_recv()
            pick(half, c, 2)
            pick(half, c, 1)
            send(4, half, c).start()
            send(5, half, c).start()
            pick(half, c, 3)
            send(6, half, c).start()
            pick(half, c, 0)
            send(7, half, c).start()

    def pass_rows(c):
        for half in (0, 1):
            for kind in (4, 5):
                send(kind, half, c).wait_recv()
                send(kind + 4, half, c).start()

    def compute(c, last):
        for half in (0, 1):
            for kind in (6, 7, 8, 9):
                send(kind, half, c).wait_recv()

        def expert(e, carry):
            mine = pl.ds(pl.multiple_of(e * slots, slots), slots)
            for dx in range(side):
                for dy in range(side):
                    at = pl.ds((dx * side + dy) * slots, slots)
                    ze[at, 0:HALF] = zb[0, c, dy, dx, mine, :]
                    ze[at, HALF:wide] = zb[1, c, dx, dy, mine, :]
            for n in range(parts):
                step = (c * experts + e) * parts + n

                @pl.when(step + 2 < steps)
                def _():
                    for copy in weights(step + 2):
                        copy.start()

                for copy in weights(step):
                    copy.wait()
                slot = step % 3
                if last:

                    @pl.when(e > 0)
                    def _():
                        result(e - 1, n).wait()

                def tile(t, carry):
                    at = pl.ds(pl.multiple_of(t * 256, 256), 256)
                    to = pl.ds(pl.multiple_of(n * part + t * 256, 256), 256)
                    g = accg[e, :, to] + dot(ze[...], wgb[slot, :, at])
                    u = accu[e, :, to] + dot(ze[...], wub[slot, :, at])
                    if last:
                        hst[n, :, at] = (jax.nn.silu(g) * u).astype(BF16)
                    else:
                        accg[e, :, to] = g
                        accu[e, :, to] = u
                    return carry

                lax.fori_loop(0, part // 256, tile, 0)
                if last:
                    result(e, n).start()
            return carry

        lax.fori_loop(0, experts, expert, 0)

    def result(e, n):
        return pltpu.make_async_copy(hst.at[n], h_hbm.at[e, :, pl.ds(n * part, part)], hs.at[n])

    own_blocks(0)
    for half in (0, 1):
        for d in hops:
            routing(half, d).start()
    own_blocks(1)

    def clear(i, carry):
        at = pl.ds(pl.multiple_of(i * 128, 128), 128)
        for e in range(experts):
            accg[e, :, at] = jnp.zeros((accg.shape[1], 128), F32)
            accu[e, :, at] = jnp.zeros((accg.shape[1], 128), F32)
        return carry

    pass_blocks(0)
    lax.fori_loop(0, ff // 128, clear, 0)
    for half in (0, 1):
        for d in hops:
            routing(half, d).wait_recv()
        for r in range(side):
            for j in range(side):
                base = place.second(half, j) * rows
                dm[half, j, r] = hits(rtb[half, r], base, rows, tokens, False).astype(BF16)
    relay(0)
    pass_blocks(1)
    own_blocks(2)

    def chunk(c, carry):
        pass_rows(c)
        relay(c + 1)

        @pl.when(c + 2 < chunks)
        def _():
            pass_blocks(c + 2)

        @pl.when(c + 3 < chunks)
        def _():
            own_blocks(c + 3)

        compute(c, False)
        return carry

    lax.fori_loop(0, chunks - 1, chunk, 0)
    pass_rows(chunks - 1)
    compute(chunks - 1, True)
    for n in range(parts):
        result(experts - 1, n).wait()
    rt_out[...] = rtb[...]

    def drain(c, carry):
        for half in (0, 1):
            for kind in (0, 1, 2, 3, 8, 9):
                send(kind, half, c).wait_send()
        return carry

    lax.fori_loop(0, chunks, drain, 0)
    for half in (0, 1):
        for kind in (4, 5, 6, 7):
            send(kind, half, chunks - 1).wait_send()
        for d in hops:
            routing(half, d).wait_send()


def expert_out(side, slots, chunks, rt_ref, x_ref, h_hbm, wd_hbm, sg_hbm, su_hbm, sd_hbm, y_ref,
               hb, wdb, ob, rb, tran, cm, summed, hs, hr, ss, sr, yacc, sgb, sub, sdb, hsb,
               ps, pr, ws, hsem, ssem):
    place = Place(side)
    tokens = x_ref.shape[0]
    rows = ob.shape[4]
    experts = hb.shape[0]
    ff = hsb.shape[1]
    wide = 2 * HALF
    steps = chunks * experts
    half_rows = tokens // 2
    low, high = pl.ds(0, half_rows), pl.ds(half_rows, half_rows)

    barrier = pltpu.get_barrier_semaphore()
    for half in (0, 1):
        for d in (1, -1):
            pl.semaphore_signal(barrier, inc=1, device_id={"ep": place.first(half, d)}, device_id_type=MESH)

    def load_h(e):
        return pltpu.make_async_copy(h_hbm.at[e], hb.at[e], hsem.at[e])

    def weights(step):
        slot = step % 2
        c, e = step // experts, step % experts
        return pltpu.make_async_copy(
            wd_hbm.at[e, :, pl.ds(pl.multiple_of(c * wide, wide), wide)], wdb.at[slot], ws.at[slot])

    load_h(0).start()
    weights(0).start()
    for e in range(1, experts):
        load_h(e).start()

    def send(kind, half, c):
        plus, minus = (1, -1)
        par = c % 2
        src, dst, to = [
            lambda: (ob.at[half, par, 2, pl.ds(0, 2)], tran.at[half, c, 0], place.second(half, plus)),
            lambda: (ob.at[half, par, 2, pl.ds(2, 2)], tran.at[half, c, 1], place.second(half, minus)),
            lambda: (ob.at[half, par, 1], rb.at[half, c, 2], place.second(half, plus)),
            lambda: (ob.at[half, par, 3], rb.at[half, c, 0], place.second(half, minus)),
            lambda: (tran.at[half, c, 0], rb.at[half, c, 1, pl.ds(0, 2)], place.second(half, plus)),
            lambda: (tran.at[half, c, 1], rb.at[half, c, 1, pl.ds(2, 2)], place.second(half, minus)),
            lambda: (hs.at[half, 0], hr.at[half, c, 0], place.first(half, plus)),
            lambda: (hs.at[half, 1], hr.at[half, c, 1], place.first(half, minus)),
            lambda: (ss.at[half, 0], sr.at[half, c, 0], place.first(half, plus)),
            lambda: (ss.at[half, 1], sr.at[half, c, 1], place.first(half, minus)),
        ][kind]()
        return pltpu.make_async_remote_copy(
            src_ref=src, dst_ref=dst, send_sem=ps.at[kind, half, c], recv_sem=pr.at[kind, half, c],
            device_id={"ep": to}, device_id_type=MESH)

    def down(c):
        par = c % 2

        def expert(e, carry):
            step = c * experts + e

            @pl.when(step + 1 < steps)
            def _():
                weights(step + 1).start()

            weights(step).wait()
            mine = pl.ds(pl.multiple_of(e * slots, slots), slots)
            for half in (0, 1):
                out = dot(hb[e], wdb[step % 2, :, half * HALF : (half + 1) * HALF]).astype(BF16)
                for dx in range(side):
                    for dy in range(side):
                        j, r = (dy, dx) if half == 0 else (dx, dy)
                        at = (dx * side + dy) * slots
                        ob[half, par, j, r, mine, :] = out[at : at + slots]
            return carry

        lax.fori_loop(0, experts, expert, 0)

    def send_rows(c):
        for half in (0, 1):
            for kind in (0, 1, 2, 3):
                send(kind, half, c).start()

    def pass_rows(c):
        for half in (0, 1):
            for kind in (0, 1):
                send(kind, half, c).wait_recv()
                send(kind + 4, half, c).start()

    def relay(c):
        par = c % 2
        for half in (0, 1):
            for kind in (2, 3, 4, 5):
                send(kind, half, c).wait_recv()

            def total(r):
                out = dot(cm[half, 0, r], ob[half, par, 0, r])
                for j in range(1, side):
                    out = out + dot(cm[half, j, r], rb[half, c, j - 1, r])
                return out

            far = total(2).astype(BF16)

            @pl.when(c > 0)
            def _():
                for kind in (6, 7):
                    send(kind, half, c - 1).wait_send()

            hs[half, 0] = far[:half_rows]
            hs[half, 1] = far[half_rows:]
            summed[half, 0] = total(1)
            send(6, half, c).start()
            summed[half, 1] = total(3)
            send(7, half, c).start()
            at = pl.ds(pl.multiple_of(c * wide + half * HALF, HALF), HALF)
            yacc[:, at] += total(0)

    def near(c):
        for half in (0, 1):

            @pl.when(c > 0)
            def _():
                for kind in (8, 9):
                    send(kind, half, c - 1).wait_send()

            send(6, half, c).wait_recv()
            ss[half, 0, low] = (summed[half, 0, low] + hr[half, c, 0].astype(F32)).astype(BF16)
            ss[half, 0, high] = summed[half, 0, high].astype(BF16)
            send(7, half, c).wait_recv()
            ss[half, 1, low] = summed[half, 1, low].astype(BF16)
            ss[half, 1, high] = (summed[half, 1, high] + hr[half, c, 1].astype(F32)).astype(BF16)
            send(8, half, c).start()
            send(9, half, c).start()

    def finish(c):
        for half in (0, 1):
            for kind in (8, 9):
                send(kind, half, c).wait_recv()
            at = pl.ds(pl.multiple_of(c * wide + half * HALF, HALF), HALF)
            total = yacc[:, at] + sr[half, c, 0].astype(F32) + sr[half, c, 1].astype(F32)
            y_ref[:, at] = total.astype(BF16)

    def shared_in(n):
        at = pl.ds(pl.multiple_of(n * 256, 256), 256)
        return (
            pltpu.make_async_copy(sg_hbm.at[:, at], sgb.at[n % 2], ssem.at[0, n % 2]),
            pltpu.make_async_copy(su_hbm.at[:, at], sub.at[n % 2], ssem.at[1, n % 2]),
        )

    def shared_out(n):
        at = pl.ds(pl.multiple_of(n * wide, wide), wide)
        return pltpu.make_async_copy(sd_hbm.at[:, at], sdb.at[n % 2], ssem.at[2, n % 2])

    def shared():
        def inner(n, carry):
            @pl.when(n + 1 < ff // 256)
            def _():
                for copy in shared_in(n + 1):
                    copy.start()

            for copy in shared_in(n):
                copy.wait()
            g = dot(x_ref[...], sgb[n % 2])
            u = dot(x_ref[...], sub[n % 2])
            hsb[:, pl.ds(pl.multiple_of(n * 256, 256), 256)] = (jax.nn.silu(g) * u).astype(BF16)
            return carry

        lax.fori_loop(0, ff // 256, inner, 0)

        def outer(n, carry):
            @pl.when(n + 1 < chunks)
            def _():
                shared_out(n + 1).start()

            shared_out(n).wait()
            yacc[:, pl.ds(pl.multiple_of(n * wide, wide), wide)] = dot(hsb[...], sdb[n % 2])
            return carry

        lax.fori_loop(0, chunks, outer, 0)

    for e in range(experts):
        load_h(e).wait()
    down(0)
    pl.semaphore_wait(barrier, 4)
    send_rows(0)
    for copy in shared_in(0):
        copy.start()
    shared_out(0).start()
    for half in (0, 1):
        for r in range(side):
            for j in range(side):
                base = place.second(half, j) * rows
                cm[half, j, r] = hits(rt_ref[half, r], base, rows, tokens, True).T.astype(BF16)
    pass_rows(0)
    down(1)
    send_rows(1)
    shared()

    def chunk(c, carry):
        @pl.when(c > 0)
        def _():
            near(c - 1)

        relay(c)

        @pl.when(c + 1 < chunks)
        def _():
            pass_rows(c + 1)

        @pl.when(c + 2 < chunks)
        def _():
            for half in (0, 1):
                for kind in (0, 1, 2, 3):
                    send(kind, half, c).wait_send()
            down(c + 2)
            send_rows(c + 2)

        @pl.when(c > 1)
        def _():
            finish(c - 2)

        return carry

    lax.fori_loop(0, chunks, chunk, 0)
    near(chunks - 1)
    finish(chunks - 2)
    finish(chunks - 1)

    for half in (0, 1):
        for kind in (6, 7, 8, 9):
            send(kind, half, chunks - 1).wait_send()
        for c in (chunks - 2, chunks - 1):
            for kind in (0, 1, 2, 3):
                send(kind, half, c).wait_send()

    def drain(c, carry):
        for half in (0, 1):
            for kind in (4, 5):
                send(kind, half, c).wait_send()
        return carry

    lax.fori_loop(0, chunks, drain, 0)


def solution(mesh):
    members = mesh.shape["ep"]
    side = math.isqrt(members)

    def local(x, expert, slot, gate, w_gate, w_up, w_down, s_gate, s_up, s_down):
        x, expert, slot, gate = x[0, 0], expert[0, 0], slot[0, 0], gate[0, 0]
        (tokens, top), (experts, d, ff) = expert.shape, w_gate.shape
        slots = 5 * tokens * top // (4 * experts * members)
        rows, wide = experts * slots, 2 * HALF
        chunks = d // wide
        part = ff // 2
        key = jnp.where(slot < slots, expert * slots + slot, -1).astype(F32)
        weight = gate.astype(BF16).astype(F32)
        rt = jnp.concatenate([key.T, weight.T], axis=0)

        vmem, anywhere = pl.BlockSpec(memory_space=pltpu.VMEM), pl.BlockSpec(memory_space=pl.ANY)
        dma = pltpu.SemaphoreType.DMA

        def buf(*shape, dtype=BF16):
            return pltpu.VMEM(shape, dtype)

        h, rt_all = pl.pallas_call(
            functools.partial(expert_in, side, slots, chunks),
            out_shape=(
                jax.ShapeDtypeStruct((experts, members * slots, ff), BF16),
                jax.ShapeDtypeStruct((2, side, 2 * top, tokens), F32),
            ),
            in_specs=[vmem, vmem, anywhere, anywhere],
            out_specs=(anywhere, vmem),
            scratch_shapes=[
                buf(2, side, 2 * top, tokens, dtype=F32),
                buf(2, chunks, 3, tokens, HALF),
                buf(2, chunks, 2, 2, rows, HALF),
                buf(2, 3, side, rows, HALF),
                buf(2, chunks, side, side, rows, HALF),
                buf(2, side, side, rows, tokens),
                buf(3, wide, part),
                buf(3, wide, part),
                buf(experts, members * slots, ff, dtype=F32),
                buf(experts, members * slots, ff, dtype=F32),
                buf(members * slots, wide),
                buf(2, members * slots, part),
                dma((2, side)),
                dma((2, side)),
                dma((10, 2, chunks)),
                dma((10, 2, chunks)),
                dma((2, 3)),
                dma((2,)),
            ],
            compiler_params=pltpu.CompilerParams(collective_id=0, has_side_effects=True, vmem_limit_bytes=VMEM_BYTES),
            name="expert_in",
        )(rt, x, w_gate, w_up)

        y = pl.pallas_call(
            functools.partial(expert_out, side, slots, chunks),
            out_shape=jax.ShapeDtypeStruct((tokens, d), BF16),
            in_specs=[vmem, vmem] + [anywhere] * 5,
            out_specs=vmem,
            scratch_shapes=[
                buf(experts, members * slots, ff),
                buf(2, ff, wide),
                buf(2, 2, side, side, rows, HALF),
                buf(2, chunks, 3, side, rows, HALF),
                buf(2, chunks, 2, 2, rows, HALF),
                buf(2, side, side, tokens, rows),
                buf(2, 2, tokens, HALF, dtype=F32),
                buf(2, 2, tokens // 2, HALF),
                buf(2, chunks, 2, tokens // 2, HALF),
                buf(2, 2, tokens, HALF),
                buf(2, chunks, 2, tokens, HALF),
                buf(tokens, d, dtype=F32),
                buf(2, d, 256),
                buf(2, d, 256),
                buf(2, ff, wide),
                buf(tokens, ff),
                dma((10, 2, chunks)),
                dma((10, 2, chunks)),
                dma((2,)),
                dma((experts,)),
                dma((3, 2)),
            ],
            compiler_params=pltpu.CompilerParams(collective_id=1, has_side_effects=True, vmem_limit_bytes=VMEM_BYTES),
            name="expert_out",
        )(rt_all, x, h, w_down, s_gate, s_up, s_down)
        return y[None, None]

    tok = P("dp", "ep", None, None)
    return jax.shard_map(
        local,
        mesh=mesh,
        in_specs=(tok, tok, tok, tok, P("ep"), P("ep"), P("ep"), P(), P(), P()),
        out_specs=tok,
        check_vma=False,
    )
```

time: 518 us -> 256 us (0.49)
  Pallas kernels: 0 us -> 250 us
  waiting for transfers between devices: 198 us -> 0 us
  blocking collectives: 169 us -> 0 us
  matrix products: 129 us -> 0 us
  local copies, waits for them, and re-layouts: 15.7 us -> 2.46 us
  starting transfers between devices: 5.71 us -> 0 us
    pallas_call x0 -> x2, Pallas kernels: none -> 250 us  [the longest x1 138 us: local(): pl.pallas_call(functools.partial(expert_in, side, slots, chunks), out_sha...]
    another operation x1 -> x0, waiting for transfers between devices: 198 us -> none  [placed(): return lax.with_sharding_constraint(v, NamedSharding(mesh, P(*spec)))]
    another operation x1 -> x0, blocking collectives: 169 us -> none  [placed(): return lax.with_sharding_constraint(v, NamedSharding(mesh, P(*spec)))]
    dot_general x9 -> x0, matrix products: 129 us -> none  [einsum(): return jnp.einsum(form, a.astype(jnp.float32), b.astype(jnp.float32))]
    convert_element_type x3 -> x0, local copies, waits for them, and re-layouts: 6.78 us -> none  [the longest x1 3.62 us: step(): einsum('abtke,abtkc->abtec', weighted, to_slot).astype(jnp.bfloat16)]
    another operation x1 -> x0, local copies, waits for them, and re-layouts: 6.5 us -> none  [placed(): return lax.with_sharding_constraint(v, NamedSharding(mesh, P(*spec)))]
    another operation x1 -> x0, starting transfers between devices: 5.71 us -> none  [placed(): return lax.with_sharding_constraint(v, NamedSharding(mesh, P(*spec)))]
  transfers between devices with their start and end apart: 1 -> 0, of which waited for: 1 -> 0; matrix products, arithmetic and copies ran while one was open for 5% -> 0% of each run, Pallas kernels for 0% -> 0%
where the time goes in v1:
time: 256 us; the launch traced here: 255 us
  Pallas kernels  250 us (98%)
    pallas_call x1, Pallas kernels, local(): pl.pallas_call(functools.partial(expert_in, side, slots, chunks), out_sha...  138 us
    pallas_call x1, Pallas kernels, local(): pl.pallas_call(functools.partial(expert_out, side, slots, chunks), out_sh...  113 us

profile of v1, /device:TPU:96, one launch (start us, length us, event | category | flops | bytes accessed | tf_op | source)
XLA Modules:
  0.0 254.8 jit_solution(8825173921044558358)
XLA Ops:
  0.0 0.7 convert_bitcast_fusion.1
  0.7 0.7 convert_bitcast_fusion
  1.4 0.6 pad_maximum_fusion.rt_ref
  2.0 137.6 %expert_in.1 = (bf16[5,512,1536]{2,1,0:T(8,128)(2,1)}, f32[2,4,16,256]{3,2,1,0:T(8,128)}) custom-call(f32[16,256]{1,0:T(8,128)} %pad_maximum_fusion.rt_ref, bf16[256,2560]{1,0:T(8,128)(2,1)} %bitcast.12, bf16[5,2560,1536]{2,1,0:T(8,128)(2,1)} %wg_hbm.1, bf16[5,2560,1536]{2,1,0:T(8,128)(2,1)} %wu_hbm.1), custom_call_target="tpu_custom_call" | custom-call | tf_op jit(solution)/shard_map/expert_in/pallas_call | solution.py:528
  139.6 112.7 %expert_out.1 = bf16[256,2560]{1,0:T(8,128)(2,1)} custom-call(f32[2,4,16,256]{3,2,1,0:T(8,128)} %get-tuple-element.7.rt_ref, bf16[256,2560]{1,0:T(8,128)(2,1)} %bitcast.13, bf16[5,512,1536]{2,1,0:T(8,128)(2,1)} %get-tuple-element.8.h_hbm, bf16[5,1536,2560]{2,1,0:T(8,128)(2,1)} %wd_hbm.1, bf16[2560,1536]{1,0:T(8,128)(2,1)} %sg_hbm.1, ...), custom_call_target="tpu_custom_call" | custom-call | tf_op jit(solution)/shard_map/expert_out/pallas_call | solution.py:560
  252.3 2.5 copy.12

commit v2 on v1

--- a/solution.py
+++ b/solution.py
@@ -126,24 +126,22 @@
             else:
                 pk[half, j - 1, r] = rows_out
 
-    def relay(c):
-        for half in (0, 1):
-
-            @pl.when(c > 0)
-            def _():
-                for kind in (4, 5, 6, 7):
-                    send(kind, half, c - 1).wait_send()
-
-            send(2, half, c).wait_recv()
-            send(3, half, c).wait_recv()
-            pick(half, c, 2)
-            pick(half, c, 1)
-            send(4, half, c).start()
-            send(5, half, c).start()
-            pick(half, c, 3)
-            send(6, half, c).start()
-            pick(half, c, 0)
-            send(7, half, c).start()
+    def relay(half, c):
+        @pl.when(c > 0)
+        def _():
+            for kind in (4, 5, 6, 7):
+                send(kind, half, c - 1).wait_send()
+
+        send(2, half, c).wait_recv()
+        send(3, half, c).wait_recv()
+        pick(half, c, 2)
+        pick(half, c, 1)
+        send(4, half, c).start()
+        send(5, half, c).start()
+        pick(half, c, 3)
+        send(6, half, c).start()
+        pick(half, c, 0)
+        send(7, half, c).start()
 
     def pass_rows(c):
         for half in (0, 1):
@@ -151,11 +149,12 @@
                 send(kind, half, c).wait_recv()
                 send(kind + 4, half, c).start()
 
-    def compute(c, last):
+    def arrive(c):
         for half in (0, 1):
             for kind in (6, 7, 8, 9):
                 send(kind, half, c).wait_recv()
 
+    def compute(c, first, end, last):
         def expert(e, carry):
             mine = pl.ds(pl.multiple_of(e * slots, slots), slots)
             for dx in range(side):
@@ -163,7 +162,8 @@
                     at = pl.ds((dx * side + dy) * slots, slots)
                     ze[at, 0:HALF] = zb[0, c, dy, dx, mine, :]
                     ze[at, HALF:wide] = zb[1, c, dx, dy, mine, :]
-            for n in range(parts):
+
+            def columns(n, carry):
                 step = (c * experts + e) * parts + n
 
                 @pl.when(step + 2 < steps)
@@ -180,8 +180,8 @@
                     def _():
                         result(e - 1, n).wait()
 
-                def tile(t, carry):
-                    at = pl.ds(pl.multiple_of(t * 256, 256), 256)
+                for t in range(part // 256):
+                    at = pl.ds(t * 256, 256)
                     to = pl.ds(pl.multiple_of(n * part + t * 256, 256), 256)
                     g = accg[e, :, to] + dot(ze[...], wgb[slot, :, at])
                     u = accu[e, :, to] + dot(ze[...], wub[slot, :, at])
@@ -190,17 +190,16 @@
                     else:
                         accg[e, :, to] = g
                         accu[e, :, to] = u
-                    return carry
-
-                lax.fori_loop(0, part // 256, tile, 0)
                 if last:
                     result(e, n).start()
-            return carry
-
-        lax.fori_loop(0, experts, expert, 0)
+                return carry
+
+            return lax.fori_loop(0, parts, columns, carry)
+
+        lax.fori_loop(first, end, expert, 0)
 
     def result(e, n):
-        return pltpu.make_async_copy(hst.at[n], h_hbm.at[e, :, pl.ds(n * part, part)], hs.at[n])
+        return pltpu.make_async_copy(hst.at[n], h_hbm.at[e, :, pl.ds(pl.multiple_of(n * part, part), part)], hs.at[n])
 
     own_blocks(0)
     for half in (0, 1):
@@ -224,28 +223,48 @@
             for j in range(side):
                 base = place.second(half, j) * rows
                 dm[half, j, r] = hits(rtb[half, r], base, rows, tokens, False).astype(BF16)
-    relay(0)
+    relay(0, 0)
+    relay(1, 0)
     pass_blocks(1)
     own_blocks(2)
 
     def chunk(c, carry):
         pass_rows(c)
-        relay(c + 1)
+
+        @pl.when(c + 1 < chunks)
+        def _():
+            relay(0, c + 1)
+
+        @pl.when(c > 0)
+        def _():
+            arrive(c - 1)
+            compute(c - 1, 0, 2, False)
+
+        @pl.when(c + 1 < chunks)
+        def _():
+            relay(1, c + 1)
+
+        @pl.when(c > 0)
+        def _():
+            compute(c - 1, 2, 3, False)
 
         @pl.when(c + 2 < chunks)
         def _():
             pass_blocks(c + 2)
 
+        @pl.when(c > 0)
+        def _():
+            compute(c - 1, 3, experts, False)
+
         @pl.when(c + 3 < chunks)
         def _():
             own_blocks(c + 3)
 
-        compute(c, False)
         return carry
 
-    lax.fori_loop(0, chunks - 1, chunk, 0)
-    pass_rows(chunks - 1)
-    compute(chunks - 1, True)
+    lax.fori_loop(0, chunks, chunk, 0)
+    arrive(chunks - 1)
+    compute(chunks - 1, 0, experts, True)
     for n in range(parts):
         result(experts - 1, n).wait()
     rt_out[...] = rtb[...]
@@ -315,7 +334,7 @@
             src_ref=src, dst_ref=dst, send_sem=ps.at[kind, half, c], recv_sem=pr.at[kind, half, c],
             device_id={"ep": to}, device_id_type=MESH)
 
-    def down(c):
+    def down(c, loading=False):
         par = c % 2
 
         def expert(e, carry):
@@ -326,6 +345,8 @@
                 weights(step + 1).start()
 
             weights(step).wait()
+            if loading:
+                load_h(e).wait()
             mine = pl.ds(pl.multiple_of(e * slots, slots), slots)
             for half in (0, 1):
                 out = dot(hb[e], wdb[step % 2, :, half * HALF : (half + 1) * HALF]).astype(BF16)
@@ -440,9 +461,7 @@
 
         lax.fori_loop(0, chunks, outer, 0)
 
-    for e in range(experts):
-        load_h(e).wait()
-    down(0)
+    down(0, True)
     pl.semaphore_wait(barrier, 4)
     send_rows(0)
     for copy in shared_in(0):

time: 256 us -> 247 us (0.965)
  Pallas kernels: 250 us -> 241 us
    pallas_call x1, Pallas kernels: 138 us -> 128 us  [local(): pl.pallas_call(functools.partial(expert_in, side, slots, chunks), out_sha...]
where the time goes in v2:
time: 247 us; the launch traced here: 246 us
  Pallas kernels  241 us (98%)
    pallas_call x1, Pallas kernels, local(): pl.pallas_call(functools.partial(expert_in, side, slots, chunks), out_sha...  128 us
    pallas_call x1, Pallas kernels, local(): pl.pallas_call(functools.partial(expert_out, side, slots, chunks), out_sh...  114 us

profile of v2, /device:TPU:96, one launch (start us, length us, event | category | flops | bytes accessed | tf_op | source)
XLA Modules:
  0.0 245.9 jit_solution(3561287565347293764)
XLA Ops:
  0.0 0.7 convert_bitcast_fusion.1
  0.7 0.7 convert_bitcast_fusion
  1.4 0.6 pad_maximum_fusion.rt_ref
  2.0 127.8 %expert_in.1 = (bf16[5,512,1536]{2,1,0:T(8,128)(2,1)}, f32[2,4,16,256]{3,2,1,0:T(8,128)}) custom-call(f32[16,256]{1,0:T(8,128)} %pad_maximum_fusion.rt_ref, bf16[256,2560]{1,0:T(8,128)(2,1)} %bitcast.12, bf16[5,2560,1536]{2,1,0:T(8,128)(2,1)} %wg_hbm.1, bf16[5,2560,1536]{2,1,0:T(8,128)(2,1)} %wu_hbm.1), custom_call_target="tpu_custom_call" | custom-call | tf_op jit(solution)/shard_map/expert_in/pallas_call | solution.py:547
  129.8 113.6 %expert_out.1 = bf16[256,2560]{1,0:T(8,128)(2,1)} custom-call(f32[2,4,16,256]{3,2,1,0:T(8,128)} %get-tuple-element.7.rt_ref, bf16[256,2560]{1,0:T(8,128)(2,1)} %bitcast.13, bf16[5,512,1536]{2,1,0:T(8,128)(2,1)} %get-tuple-element.8.h_hbm, bf16[5,1536,2560]{2,1,0:T(8,128)(2,1)} %wd_hbm.1, bf16[2560,1536]{1,0:T(8,128)(2,1)} %sg_hbm.1, ...), custom_call_target="tpu_custom_call" | custom-call | tf_op jit(solution)/shard_map/expert_out/pallas_call | solution.py:579
  243.4 2.5 copy.12

commit v3 on v2

--- a/solution.py
+++ b/solution.py
@@ -30,8 +30,20 @@
     def first(self, half, d):
         return self.at(d, 0) if half == 0 else self.at(0, d)
 
+    def both(self, half, first, second):
+        return self.at(first, second) if half == 0 else self.at(second, first)
+
     def second(self, half, d):
         return self.at(0, d) if half == 0 else self.at(d, 0)
+
+
+def turn(r):
+    return 1 if r < 2 else -1
+
+
+def pairs(place, half, i, r):
+    j = (0, -turn(r), 0, turn(r))[i]
+    return (0 if i < 2 else 1, r), place.second(half, j)
 
 
 def hits(rt, base, rows, tokens, weighted):
@@ -45,21 +57,21 @@
 
 
 def expert_in(side, slots, chunks, rt_ref, x_ref, wg_hbm, wu_hbm, h_hbm, rt_out,
-              rtb, raw, tran, pk, zb, dm, wgb, wub, accg, accu, ze, hst,
+              rtb, raw, nraw, pk, fw, zl, zb, dm, wgb, wub, accg, accu, ze, hst,
               rs, rr, ps, pr, ws, hs):
     place = Place(side)
-    tokens, rows = x_ref.shape[0], dm.shape[3]
+    tokens, rows = x_ref.shape[0], dm.shape[3] // 2
     experts, _, ff = accg.shape
     wide = 2 * HALF
     part = wgb.shape[2]
     parts = ff // part
     steps = chunks * experts * parts
-    hops = range(1, side)
 
     barrier = pltpu.get_barrier_semaphore()
-    for half in (0, 1):
-        for d in hops:
-            pl.semaphore_signal(barrier, inc=1, device_id={"ep": place.first(half, d)}, device_id_type=MESH)
+    for dx in range(side):
+        for dy in range(side):
+            if (dx, dy) != (0, 0):
+                pl.semaphore_signal(barrier, inc=1, device_id={"ep": place.at(dx, dy)}, device_id_type=MESH)
 
     def weights(step):
         slot = step % 3
@@ -74,13 +86,16 @@
         for copy in weights(step):
             copy.start()
     for half in (0, 1):
-        rtb[half, 0] = rt_ref[...]
-    pl.semaphore_wait(barrier, 2 * (side - 1))
-
-    def routing(half, d):
+        rtb[half, 0, 0] = rt_ref[...]
+    pl.semaphore_wait(barrier, side * side - 1)
+
+    def routing(half, g, r):
+        across = 0 if g == 0 else turn(r)
         return pltpu.make_async_remote_copy(
-            src_ref=rt_ref, dst_ref=rtb.at[half, side - d], send_sem=rs.at[half, d], recv_sem=rr.at[half, side - d],
-            device_id={"ep": place.first(half, d)}, device_id_type=MESH)
+            src_ref=rt_ref, dst_ref=rtb.at[half, g, r], send_sem=rs.at[half, g, r], recv_sem=rr.at[half, g, r],
+            device_id={"ep": place.both(half, -r, across)}, device_id_type=MESH)
+
+    routes = [(half, g, r) for g in (0, 1) for half in (0, 1) for r in range(side) if (g, r) != (0, 0)]
 
     def cols(half, c):
         return pl.ds(pl.multiple_of(c * wide + half * HALF, HALF), HALF)
@@ -94,12 +109,14 @@
             lambda: (x_ref.at[:, cols(half, c)], raw.at[half, c, 0], place.first(half, minus)),
             lambda: (raw.at[half, c, 2, low], raw.at[half, c, 1, low], place.first(half, plus)),
             lambda: (raw.at[half, c, 0, high], raw.at[half, c, 1, high], place.first(half, minus)),
-            lambda: (pk.at[half, 1, pl.ds(0, 2)], tran.at[half, c, 0], place.second(half, plus)),
-            lambda: (pk.at[half, 1, pl.ds(2, 2)], tran.at[half, c, 1], place.second(half, minus)),
-            lambda: (pk.at[half, 0], zb.at[half, c, 3], place.second(half, plus)),
-            lambda: (pk.at[half, 2], zb.at[half, c, 1], place.second(half, minus)),
-            lambda: (tran.at[half, c, 0], zb.at[half, c, 2, pl.ds(0, 2)], place.second(half, plus)),
-            lambda: (tran.at[half, c, 1], zb.at[half, c, 2, pl.ds(2, 2)], place.second(half, minus)),
+            lambda: (x_ref.at[:, cols(half, c)], nraw.at[half, c, 0, 0], place.second(half, plus)),
+            lambda: (raw.at[half, c, 0], nraw.at[half, c, 0, 1], place.second(half, plus)),
+            lambda: (raw.at[half, c, 1], nraw.at[half, c, 1, 0], place.second(half, minus)),
+            lambda: (raw.at[half, c, 2], nraw.at[half, c, 1, 1], place.second(half, minus)),
+            lambda: (pk.at[half, pl.ds(0, 2)], zb.at[half, c, 0, pl.ds(0, 2)], place.second(half, minus)),
+            lambda: (pk.at[half, pl.ds(2, 2)], zb.at[half, c, 2, pl.ds(2, 2)], place.second(half, plus)),
+            lambda: (fw.at[half, pl.ds(0, 2)], zb.at[half, c, 1, pl.ds(0, 2)], place.second(half, plus)),
+            lambda: (fw.at[half, pl.ds(2, 2)], zb.at[half, c, 1, pl.ds(2, 2)], place.second(half, minus)),
         ][kind]()
         return pltpu.make_async_remote_copy(
             src_ref=src, dst_ref=dst, send_sem=ps.at[kind, half, c], recv_sem=pr.at[kind, half, c],
@@ -109,6 +126,8 @@
         for half in (0, 1):
             send(0, half, c).start()
             send(1, half, c).start()
+        for half in (0, 1):
+            send(4, half, c).start()
 
     def pass_blocks(c):
         for half in (0, 1):
@@ -116,42 +135,47 @@
             send(2, half, c).start()
             send(1, half, c).wait_recv()
             send(3, half, c).start()
-
-    def pick(half, c, j):
-        for r in range(side):
-            block = x_ref[:, cols(half, c)] if r == 0 else raw[half, c, r - 1]
-            rows_out = dot(dm[half, j, r], block).astype(BF16)
-            if j == 0:
-                zb[half, c, 0, r] = rows_out
-            else:
-                pk[half, j - 1, r] = rows_out
+        for half in (0, 1):
+            send(7, half, c).start()
+            send(5, half, c).start()
+
+    def pick(half, stage, r, block):
+        out = dot(dm[half, stage, r], block).astype(BF16)
+        return out[:rows], out[rows:]
+
+    def block(half, c, r):
+        return x_ref[:, cols(half, c)] if r == 0 else raw[half, c, r - 1]
 
     def relay(half, c):
         @pl.when(c > 0)
         def _():
-            for kind in (4, 5, 6, 7):
+            for kind in (8, 9):
                 send(kind, half, c - 1).wait_send()
 
         send(2, half, c).wait_recv()
         send(3, half, c).wait_recv()
-        pick(half, c, 2)
-        pick(half, c, 1)
-        send(4, half, c).start()
-        send(5, half, c).start()
-        pick(half, c, 3)
         send(6, half, c).start()
-        pick(half, c, 0)
-        send(7, half, c).start()
-
-    def pass_rows(c):
-        for half in (0, 1):
-            for kind in (4, 5):
-                send(kind, half, c).wait_recv()
-                send(kind + 4, half, c).start()
+        for r in range(side):
+            pk[half, r], zl[half, c % 3, r] = pick(half, 0, r, block(half, c, r))
+            if r >= 2:
+                send(6 + r, half, c).start()
+
+    def pass_rows(half, c):
+        @pl.when(c > 0)
+        def _():
+            for kind in (10, 11):
+                send(kind, half, c - 1).wait_send()
+
+        for kind in (4, 5, 6, 7):
+            send(kind, half, c).wait_recv()
+        for r in range(side):
+            fw[half, r], zb[half, c, 2 if r < 2 else 0, r] = pick(half, 1, r, nraw[half, c, r // 2, r % 2])
+            if r >= 2:
+                send(8 + r, half, c).start()
 
     def arrive(c):
         for half in (0, 1):
-            for kind in (6, 7, 8, 9):
+            for kind in (8, 9, 10, 11):
                 send(kind, half, c).wait_recv()
 
     def compute(c, first, end, last):
@@ -160,8 +184,8 @@
             for dx in range(side):
                 for dy in range(side):
                     at = pl.ds((dx * side + dy) * slots, slots)
-                    ze[at, 0:HALF] = zb[0, c, dy, dx, mine, :]
-                    ze[at, HALF:wide] = zb[1, c, dx, dy, mine, :]
+                    ze[at, 0:HALF] = zl[0, c % 3, dx, mine, :] if dy == 0 else zb[0, c, dy - 1, dx, mine, :]
+                    ze[at, HALF:wide] = zl[1, c % 3, dy, mine, :] if dx == 0 else zb[1, c, dx - 1, dy, mine, :]
 
             def columns(n, carry):
                 step = (c * experts + e) * parts + n
@@ -202,9 +226,8 @@
         return pltpu.make_async_copy(hst.at[n], h_hbm.at[e, :, pl.ds(pl.multiple_of(n * part, part), part)], hs.at[n])
 
     own_blocks(0)
-    for half in (0, 1):
-        for d in hops:
-            routing(half, d).start()
+    for route in routes:
+        routing(*route).start()
     own_blocks(1)
 
     def clear(i, carry):
@@ -217,19 +240,30 @@
     pass_blocks(0)
     lax.fori_loop(0, ff // 128, clear, 0)
     for half in (0, 1):
-        for d in hops:
-            routing(half, d).wait_recv()
+        for r in range(1, side):
+            routing(half, 0, r).wait_recv()
+
+    def select(half, stage):
         for r in range(side):
-            for j in range(side):
-                base = place.second(half, j) * rows
-                dm[half, j, r] = hits(rtb[half, r], base, rows, tokens, False).astype(BF16)
-    relay(0, 0)
-    relay(1, 0)
+            for n in (0, 1):
+                (g, at), device = pairs(place, half, 2 * stage + 1 - n, r)
+                dm[half, stage, r, n * rows : (n + 1) * rows] = hits(
+                    rtb[half, g, at], device * rows, rows, tokens, False).astype(BF16)
+
+    for half in (0, 1):
+        select(half, 0)
+        relay(half, 0)
     pass_blocks(1)
     own_blocks(2)
 
+    for half in (0, 1):
+        for r in range(side):
+            routing(half, 1, r).wait_recv()
+        select(half, 1)
+
     def chunk(c, carry):
-        pass_rows(c)
+        pass_rows(0, c)
+        pass_rows(1, c)
 
         @pl.when(c + 1 < chunks)
         def _():
@@ -271,20 +305,20 @@
 
     def drain(c, carry):
         for half in (0, 1):
-            for kind in (0, 1, 2, 3, 8, 9):
+            for kind in range(8):
                 send(kind, half, c).wait_send()
         return carry
 
     lax.fori_loop(0, chunks, drain, 0)
     for half in (0, 1):
-        for kind in (4, 5, 6, 7):
+        for kind in (8, 9, 10, 11):
             send(kind, half, chunks - 1).wait_send()
-        for d in hops:
-            routing(half, d).wait_send()
+    for route in routes:
+        routing(*route).wait_send()
 
 
 def expert_out(side, slots, chunks, rt_ref, x_ref, h_hbm, wd_hbm, sg_hbm, su_hbm, sd_hbm, y_ref,
-               hb, wdb, ob, rb, tran, cm, summed, hs, hr, ss, sr, yacc, sgb, sub, sdb, hsb,
+               hb, wdb, ob, rb, tran, tb, tokb, cm, summed, hs, hr, ss, sr, yacc, sgb, sub, sdb, hsb,
                ps, pr, ws, hsem, ssem):
     place = Place(side)
     tokens = x_ref.shape[0]
@@ -317,14 +351,14 @@
 
     def send(kind, half, c):
         plus, minus = (1, -1)
-        par = c % 2
+        par = c % 3
         src, dst, to = [
-            lambda: (ob.at[half, par, 2, pl.ds(0, 2)], tran.at[half, c, 0], place.second(half, plus)),
-            lambda: (ob.at[half, par, 2, pl.ds(2, 2)], tran.at[half, c, 1], place.second(half, minus)),
-            lambda: (ob.at[half, par, 1], rb.at[half, c, 2], place.second(half, plus)),
-            lambda: (ob.at[half, par, 3], rb.at[half, c, 0], place.second(half, minus)),
-            lambda: (tran.at[half, c, 0], rb.at[half, c, 1, pl.ds(0, 2)], place.second(half, plus)),
-            lambda: (tran.at[half, c, 1], rb.at[half, c, 1, pl.ds(2, 2)], place.second(half, minus)),
+            lambda: (ob.at[half, par, 2, pl.ds(0, 2)], tran.at[half, c, 0], place.second(half, minus)),
+            lambda: (ob.at[half, par, 2, pl.ds(2, 2)], tran.at[half, c, 1], place.second(half, plus)),
+            lambda: (ob.at[half, par, 1, pl.ds(0, 2)], rb.at[half, c, 0], place.second(half, plus)),
+            lambda: (ob.at[half, par, 3, pl.ds(2, 2)], rb.at[half, c, 1], place.second(half, minus)),
+            lambda: (tokb.at[half, 0], tb.at[half, c, 0], place.second(half, minus)),
+            lambda: (tokb.at[half, 1], tb.at[half, c, 1], place.second(half, plus)),
             lambda: (hs.at[half, 0], hr.at[half, c, 0], place.first(half, plus)),
             lambda: (hs.at[half, 1], hr.at[half, c, 1], place.first(half, minus)),
             lambda: (ss.at[half, 0], sr.at[half, c, 0], place.first(half, plus)),
@@ -335,7 +369,7 @@
             device_id={"ep": to}, device_id_type=MESH)
 
     def down(c, loading=False):
-        par = c % 2
+        par = c % 3
 
         def expert(e, carry):
             step = c * experts + e
@@ -365,22 +399,32 @@
                 send(kind, half, c).start()
 
     def pass_rows(c):
-        for half in (0, 1):
-            for kind in (0, 1):
-                send(kind, half, c).wait_recv()
-                send(kind + 4, half, c).start()
+        par = c % 3
+        for half in (0, 1):
+
+            @pl.when(c > 0)
+            def _():
+                for kind in (4, 5):
+                    send(kind, half, c - 1).wait_send()
+
+            for way in (0, 1):
+                send(way, half, c).wait_recv()
+                for n in range(2):
+                    r = 2 * way + n
+                    total = dot(cm[half, 2, r], ob[half, par, 3 if way == 0 else 1, r])
+                    tokb[half, way, n] = (total + dot(cm[half, 3, r], tran[half, c, way, n])).astype(BF16)
+            for way in (0, 1):
+                send(way + 4, half, c).start()
 
     def relay(c):
-        par = c % 2
+        par = c % 3
         for half in (0, 1):
             for kind in (2, 3, 4, 5):
                 send(kind, half, c).wait_recv()
 
             def total(r):
-                out = dot(cm[half, 0, r], ob[half, par, 0, r])
-                for j in range(1, side):
-                    out = out + dot(cm[half, j, r], rb[half, c, j - 1, r])
-                return out
+                out = dot(cm[half, 0, r], ob[half, par, 0, r]) + dot(cm[half, 1, r], rb[half, c, r // 2, r % 2])
+                return out + tb[half, c, r // 2, r % 2].astype(F32)
 
             far = total(2).astype(BF16)
 
@@ -434,32 +478,42 @@
         at = pl.ds(pl.multiple_of(n * wide, wide), wide)
         return pltpu.make_async_copy(sd_hbm.at[:, at], sdb.at[n % 2], ssem.at[2, n % 2])
 
-    def shared():
-        def inner(n, carry):
-            @pl.when(n + 1 < ff // 256)
+    def inner(n):
+        @pl.when(n + 1 < ff // 256)
+        def _():
+            for copy in shared_in(n + 1):
+                copy.start()
+
+        for copy in shared_in(n):
+            copy.wait()
+        g = dot(x_ref[...], sgb[n % 2])
+        u = dot(x_ref[...], sub[n % 2])
+        hsb[:, pl.ds(pl.multiple_of(n * 256, 256), 256)] = (jax.nn.silu(g) * u).astype(BF16)
+
+    def outer(n):
+        @pl.when(n + 1 < chunks)
+        def _():
+            shared_out(n + 1).start()
+
+        shared_out(n).wait()
+        yacc[:, pl.ds(pl.multiple_of(n * wide, wide), wide)] += dot(hsb[...], sdb[n % 2])
+
+    pieces = ff // 256 + chunks
+    per = -(-pieces // (chunks - 1))
+
+    def shared(c):
+        def piece(p, carry):
+            @pl.when(p < ff // 256)
             def _():
-                for copy in shared_in(n + 1):
-                    copy.start()
-
-            for copy in shared_in(n):
-                copy.wait()
-            g = dot(x_ref[...], sgb[n % 2])
-            u = dot(x_ref[...], sub[n % 2])
-            hsb[:, pl.ds(pl.multiple_of(n * 256, 256), 256)] = (jax.nn.silu(g) * u).astype(BF16)
+                inner(p)
+
+            @pl.when((p >= ff // 256) & (p < pieces))
+            def _():
+                outer(p - ff // 256)
+
             return carry
 
-        lax.fori_loop(0, ff // 256, inner, 0)
-
-        def outer(n, carry):
-            @pl.when(n + 1 < chunks)
-            def _():
-                shared_out(n + 1).start()
-
-            shared_out(n).wait()
-            yacc[:, pl.ds(pl.multiple_of(n * wide, wide), wide)] = dot(hsb[...], sdb[n % 2])
-            return carry
-
-        lax.fori_loop(0, chunks, outer, 0)
+        lax.fori_loop(c * per, c * per + per, piece, 0)
 
     down(0, True)
     pl.semaphore_wait(barrier, 4)
@@ -467,15 +521,22 @@
     for copy in shared_in(0):
         copy.start()
     shared_out(0).start()
-    for half in (0, 1):
-        for r in range(side):
-            for j in range(side):
-                base = place.second(half, j) * rows
-                cm[half, j, r] = hits(rt_ref[half, r], base, rows, tokens, True).T.astype(BF16)
-    pass_rows(0)
     down(1)
     send_rows(1)
-    shared()
+
+    def select(some):
+        for half in (0, 1):
+            for i in some:
+                for r in range(side):
+                    (g, at), device = pairs(place, half, i, r)
+                    cm[half, i, r] = hits(rt_ref[half, g, at], device * rows, rows, tokens, True).T.astype(BF16)
+
+    select((2, 3))
+    pass_rows(0)
+    down(2)
+    send_rows(2)
+    select((0, 1))
+    yacc[...] = jnp.zeros(yacc.shape, F32)
 
     def chunk(c, carry):
         @pl.when(c > 0)
@@ -488,39 +549,35 @@
         def _():
             pass_rows(c + 1)
 
-        @pl.when(c + 2 < chunks)
+        @pl.when(c + 3 < chunks)
         def _():
             for half in (0, 1):
                 for kind in (0, 1, 2, 3):
                     send(kind, half, c).wait_send()
-            down(c + 2)
-            send_rows(c + 2)
-
-        @pl.when(c > 1)
-        def _():
-            finish(c - 2)
+            down(c + 3)
+            send_rows(c + 3)
+
+        @pl.when(c + 1 < chunks)
+        def _():
+            shared(c)
 
         return carry
 
     lax.fori_loop(0, chunks, chunk, 0)
     near(chunks - 1)
-    finish(chunks - 2)
-    finish(chunks - 1)
+
+    def end(c, carry):
+        finish(c)
+        return carry
+
+    lax.fori_loop(0, chunks, end, 0)
 
     for half in (0, 1):
-        for kind in (6, 7, 8, 9):
+        for kind in (4, 5, 6, 7, 8, 9):
             send(kind, half, chunks - 1).wait_send()
-        for c in (chunks - 2, chunks - 1):
+        for c in (chunks - 3, chunks - 2, chunks - 1):
             for kind in (0, 1, 2, 3):
                 send(kind, half, c).wait_send()
-
-    def drain(c, carry):
-        for half in (0, 1):
-            for kind in (4, 5):
-                send(kind, half, c).wait_send()
-        return carry
-
-    lax.fori_loop(0, chunks, drain, 0)
 
 
 def solution(mesh):
@@ -548,27 +605,29 @@
             functools.partial(expert_in, side, slots, chunks),
             out_shape=(
                 jax.ShapeDtypeStruct((experts, members * slots, ff), BF16),
-                jax.ShapeDtypeStruct((2, side, 2 * top, tokens), F32),
+                jax.ShapeDtypeStruct((2, 2, side, 2 * top, tokens), F32),
             ),
             in_specs=[vmem, vmem, anywhere, anywhere],
             out_specs=(anywhere, vmem),
             scratch_shapes=[
-                buf(2, side, 2 * top, tokens, dtype=F32),
+                buf(2, 2, side, 2 * top, tokens, dtype=F32),
                 buf(2, chunks, 3, tokens, HALF),
-                buf(2, chunks, 2, 2, rows, HALF),
+                buf(2, chunks, 2, 2, tokens, HALF),
+                buf(2, side, rows, HALF),
+                buf(2, side, rows, HALF),
                 buf(2, 3, side, rows, HALF),
-                buf(2, chunks, side, side, rows, HALF),
-                buf(2, side, side, rows, tokens),
+                buf(2, chunks, side - 1, side, rows, HALF),
+                buf(2, 2, side, 2 * rows, tokens),
                 buf(3, wide, part),
                 buf(3, wide, part),
                 buf(experts, members * slots, ff, dtype=F32),
                 buf(experts, members * slots, ff, dtype=F32),
                 buf(members * slots, wide),
                 buf(2, members * slots, part),
-                dma((2, side)),
-                dma((2, side)),
-                dma((10, 2, chunks)),
-                dma((10, 2, chunks)),
+                dma((2, 2, side)),
+                dma((2, 2, side)),
+                dma((12, 2, chunks)),
+                dma((12, 2, chunks)),
                 dma((2, 3)),
                 dma((2,)),
             ],
@@ -584,9 +643,11 @@
             scratch_shapes=[
                 buf(experts, members * slots, ff),
                 buf(2, ff, wide),
-                buf(2, 2, side, side, rows, HALF),
-                buf(2, chunks, 3, side, rows, HALF),
+                buf(2, 3, side, side, rows, HALF),
                 buf(2, chunks, 2, 2, rows, HALF),
+                buf(2, chunks, 2, 2, rows, HALF),
+                buf(2, chunks, 2, 2, tokens, HALF),
+                buf(2, 2, 2, tokens, HALF),
                 buf(2, side, side, tokens, rows),
                 buf(2, 2, tokens, HALF, dtype=F32),
                 buf(2, 2, tokens // 2, HALF),

time: 247 us -> 234 us (0.947)
  Pallas kernels: 241 us -> 229 us
    pallas_call x1, Pallas kernels: 114 us -> 103 us  [local(): pl.pallas_call(functools.partial(expert_out, side, slots, chunks), out_sh...]
where the time goes in v3:
time: 234 us
  Pallas kernels  229 us (98%)
  local copies, waits for them, and re-layouts  2.46 us (1%)
    pallas_call x1, Pallas kernels, local(): pl.pallas_call(functools.partial(expert_in, side, slots, chunks), out_sha...  126 us
    pallas_call x1, Pallas kernels, local(): pl.pallas_call(functools.partial(expert_out, side, slots, chunks), out_sh...  103 us

profile of v3, /device:TPU:96, one launch (start us, length us, event | category | flops | bytes accessed | tf_op | source)
XLA Modules:
  0.0 233.6 jit_solution(1899553269558443165)
XLA Ops:
  0.0 0.7 convert_bitcast_fusion.1
  0.7 0.7 convert_bitcast_fusion
  1.4 0.6 pad_maximum_fusion.rt_ref
  2.0 125.9 %expert_in.1 = (bf16[5,512,1536]{2,1,0:T(8,128)(2,1)}, f32[2,2,4,16,256]{4,3,2,1,0:T(8,128)}) custom-call(f32[16,256]{1,0:T(8,128)} %pad_maximum_fusion.rt_ref, bf16[256,2560]{1,0:T(8,128)(2,1)} %bitcast.12, bf16[5,2560,1536]{2,1,0:T(8,128)(2,1)} %wg_hbm.1, bf16[5,2560,1536]{2,1,0:T(8,128)(2,1)} %wu_hbm.1), custom_call_target="tpu_custom_call" | custom-call | tf_op jit(solution)/shard_map/expert_in/pallas_call | solution.py:604
  128.0 103.2 %expert_out.1 = bf16[256,2560]{1,0:T(8,128)(2,1)} custom-call(f32[2,2,4,16,256]{4,3,2,1,0:T(8,128)} %get-tuple-element.7.rt_ref, bf16[256,2560]{1,0:T(8,128)(2,1)} %bitcast.13, bf16[5,512,1536]{2,1,0:T(8,128)(2,1)} %get-tuple-element.8.h_hbm, bf16[5,1536,2560]{2,1,0:T(8,128)(2,1)} %wd_hbm.1, bf16[2560,1536]{1,0:T(8,128)(2,1)} %sg_hbm.1, ...), custom_call_target="tpu_custom_call" | custom-call | tf_op jit(solution)/shard_map/expert_out/pallas_call | solution.py:638
  231.2 2.5 %copy.12 = bf16[1,1,256,2560]{3,2,1,0:T(8,128)(2,1)} copy(bf16[1,1,256,2560]{3,2,1,0:T(8,128)(2,1)} %bitcast.11) | data formatting | bytes 2621440

commit v4 on v3

--- a/solution.py
+++ b/solution.py
@@ -12,6 +12,9 @@
 F32, BF16 = jnp.float32, jnp.bfloat16
 VMEM_BYTES = 67_000_000
 HALF = 256
+BOTH = (0, 1)
+FRONT, BACK = pl.ds(0, 2), pl.ds(2, 2)
+PLUS, MINUS = 1, -1
 
 
 def dot(a, b):
@@ -82,10 +85,10 @@
             pltpu.make_async_copy(wu_hbm.at[at], wub.at[slot], ws.at[1, slot]),
         )
 
-    for step in (0, 1):
+    for step in BOTH:
         for copy in weights(step):
             copy.start()
-    for half in (0, 1):
+    for half in BOTH:
         rtb[half, 0, 0] = rt_ref[...]
     pl.semaphore_wait(barrier, side * side - 1)
 
@@ -95,7 +98,7 @@
             src_ref=rt_ref, dst_ref=rtb.at[half, g, r], send_sem=rs.at[half, g, r], recv_sem=rr.at[half, g, r],
             device_id={"ep": place.both(half, -r, across)}, device_id_type=MESH)
 
-    routes = [(half, g, r) for g in (0, 1) for half in (0, 1) for r in range(side) if (g, r) != (0, 0)]
+    routes = [(half, g, r) for g in BOTH for half in BOTH for r in range(side) if (g, r) != (0, 0)]
 
     def cols(half, c):
         return pl.ds(pl.multiple_of(c * wide + half * HALF, HALF), HALF)
@@ -103,39 +106,38 @@
     low, high = pl.ds(0, tokens // 2), pl.ds(tokens // 2, tokens // 2)
 
     def send(kind, half, c):
-        plus, minus = (1, -1)
         src, dst, to = [
-            lambda: (x_ref.at[:, cols(half, c)], raw.at[half, c, 2], place.first(half, plus)),
-            lambda: (x_ref.at[:, cols(half, c)], raw.at[half, c, 0], place.first(half, minus)),
-            lambda: (raw.at[half, c, 2, low], raw.at[half, c, 1, low], place.first(half, plus)),
-            lambda: (raw.at[half, c, 0, high], raw.at[half, c, 1, high], place.first(half, minus)),
-            lambda: (x_ref.at[:, cols(half, c)], nraw.at[half, c, 0, 0], place.second(half, plus)),
-            lambda: (raw.at[half, c, 0], nraw.at[half, c, 0, 1], place.second(half, plus)),
-            lambda: (raw.at[half, c, 1], nraw.at[half, c, 1, 0], place.second(half, minus)),
-            lambda: (raw.at[half, c, 2], nraw.at[half, c, 1, 1], place.second(half, minus)),
-            lambda: (pk.at[half, pl.ds(0, 2)], zb.at[half, c, 0, pl.ds(0, 2)], place.second(half, minus)),
-            lambda: (pk.at[half, pl.ds(2, 2)], zb.at[half, c, 2, pl.ds(2, 2)], place.second(half, plus)),
-            lambda: (fw.at[half, pl.ds(0, 2)], zb.at[half, c, 1, pl.ds(0, 2)], place.second(half, plus)),
-            lambda: (fw.at[half, pl.ds(2, 2)], zb.at[half, c, 1, pl.ds(2, 2)], place.second(half, minus)),
+            lambda: (x_ref.at[:, cols(half, c)], raw.at[half, c, 2], place.first(half, PLUS)),
+            lambda: (x_ref.at[:, cols(half, c)], raw.at[half, c, 0], place.first(half, MINUS)),
+            lambda: (raw.at[half, c, 2, low], raw.at[half, c, 1, low], place.first(half, PLUS)),
+            lambda: (raw.at[half, c, 0, high], raw.at[half, c, 1, high], place.first(half, MINUS)),
+            lambda: (x_ref.at[:, cols(half, c)], nraw.at[half, c, 0, 0], place.second(half, PLUS)),
+            lambda: (raw.at[half, c, 0], nraw.at[half, c, 0, 1], place.second(half, PLUS)),
+            lambda: (raw.at[half, c, 1], nraw.at[half, c, 1, 0], place.second(half, MINUS)),
+            lambda: (raw.at[half, c, 2], nraw.at[half, c, 1, 1], place.second(half, MINUS)),
+            lambda: (pk.at[half, FRONT], zb.at[half, c, 0, FRONT], place.second(half, MINUS)),
+            lambda: (pk.at[half, BACK], zb.at[half, c, 2, BACK], place.second(half, PLUS)),
+            lambda: (fw.at[half, FRONT], zb.at[half, c, 1, FRONT], place.second(half, PLUS)),
+            lambda: (fw.at[half, BACK], zb.at[half, c, 1, BACK], place.second(half, MINUS)),
         ][kind]()
         return pltpu.make_async_remote_copy(
             src_ref=src, dst_ref=dst, send_sem=ps.at[kind, half, c], recv_sem=pr.at[kind, half, c],
             device_id={"ep": to}, device_id_type=MESH)
 
     def own_blocks(c):
-        for half in (0, 1):
+        for half in BOTH:
             send(0, half, c).start()
             send(1, half, c).start()
-        for half in (0, 1):
+        for half in BOTH:
             send(4, half, c).start()
 
     def pass_blocks(c):
-        for half in (0, 1):
+        for half in BOTH:
             send(0, half, c).wait_recv()
             send(2, half, c).start()
             send(1, half, c).wait_recv()
             send(3, half, c).start()
-        for half in (0, 1):
+        for half in BOTH:
             send(7, half, c).start()
             send(5, half, c).start()
 
@@ -174,7 +176,7 @@
                 send(8 + r, half, c).start()
 
     def arrive(c):
-        for half in (0, 1):
+        for half in BOTH:
             for kind in (8, 9, 10, 11):
                 send(kind, half, c).wait_recv()
 
@@ -239,24 +241,24 @@
 
     pass_blocks(0)
     lax.fori_loop(0, ff // 128, clear, 0)
-    for half in (0, 1):
+    for half in BOTH:
         for r in range(1, side):
             routing(half, 0, r).wait_recv()
 
     def select(half, stage):
         for r in range(side):
-            for n in (0, 1):
+            for n in BOTH:
                 (g, at), device = pairs(place, half, 2 * stage + 1 - n, r)
                 dm[half, stage, r, n * rows : (n + 1) * rows] = hits(
                     rtb[half, g, at], device * rows, rows, tokens, False).astype(BF16)
 
-    for half in (0, 1):
+    for half in BOTH:
         select(half, 0)
         relay(half, 0)
     pass_blocks(1)
     own_blocks(2)
 
-    for half in (0, 1):
+    for half in BOTH:
         for r in range(side):
             routing(half, 1, r).wait_recv()
         select(half, 1)
@@ -304,13 +306,13 @@
     rt_out[...] = rtb[...]
 
     def drain(c, carry):
-        for half in (0, 1):
+        for half in BOTH:
             for kind in range(8):
                 send(kind, half, c).wait_send()
         return carry
 
     lax.fori_loop(0, chunks, drain, 0)
-    for half in (0, 1):
+    for half in BOTH:
         for kind in (8, 9, 10, 11):
             send(kind, half, chunks - 1).wait_send()
     for route in routes:
@@ -331,7 +333,7 @@
     low, high = pl.ds(0, half_rows), pl.ds(half_rows, half_rows)
 
     barrier = pltpu.get_barrier_semaphore()
-    for half in (0, 1):
+    for half in BOTH:
         for d in (1, -1):
             pl.semaphore_signal(barrier, inc=1, device_id={"ep": place.first(half, d)}, device_id_type=MESH)
 
@@ -350,19 +352,18 @@
         load_h(e).start()
 
     def send(kind, half, c):
-        plus, minus = (1, -1)
         par = c % 3
         src, dst, to = [
-            lambda: (ob.at[half, par, 2, pl.ds(0, 2)], tran.at[half, c, 0], place.second(half, minus)),
-            lambda: (ob.at[half, par, 2, pl.ds(2, 2)], tran.at[half, c, 1], place.second(half, plus)),
-            lambda: (ob.at[half, par, 1, pl.ds(0, 2)], rb.at[half, c, 0], place.second(half, plus)),
-            lambda: (ob.at[half, par, 3, pl.ds(2, 2)], rb.at[half, c, 1], place.second(half, minus)),
-            lambda: (tokb.at[half, 0], tb.at[half, c, 0], place.second(half, minus)),
-            lambda: (tokb.at[half, 1], tb.at[half, c, 1], place.second(half, plus)),
-            lambda: (hs.at[half, 0], hr.at[half, c, 0], place.first(half, plus)),
-            lambda: (hs.at[half, 1], hr.at[half, c, 1], place.first(half, minus)),
-            lambda: (ss.at[half, 0], sr.at[half, c, 0], place.first(half, plus)),
-            lambda: (ss.at[half, 1], sr.at[half, c, 1], place.first(half, minus)),
+            lambda: (ob.at[half, par, 2, FRONT], tran.at[half, c, 0], place.second(half, MINUS)),
+            lambda: (ob.at[half, par, 2, BACK], tran.at[half, c, 1], place.second(half, PLUS)),
+            lambda: (ob.at[half, par, 1, FRONT], rb.at[half, c, 0], place.second(half, PLUS)),
+            lambda: (ob.at[half, par, 3, BACK], rb.at[half, c, 1], place.second(half, MINUS)),
+            lambda: (tokb.at[half, 0], tb.at[half, c, 0], place.second(half, MINUS)),
+            lambda: (tokb.at[half, 1], tb.at[half, c, 1], place.second(half, PLUS)),
+            lambda: (hs.at[half, 0], hr.at[half, c, 0], place.first(half, PLUS)),
+            lambda: (hs.at[half, 1], hr.at[half, c, 1], place.first(half, MINUS)),
+            lambda: (ss.at[half, 0], sr.at[half, c, 0], place.first(half, PLUS)),
+            lambda: (ss.at[half, 1], sr.at[half, c, 1], place.first(half, MINUS)),
         ][kind]()
         return pltpu.make_async_remote_copy(
             src_ref=src, dst_ref=dst, send_sem=ps.at[kind, half, c], recv_sem=pr.at[kind, half, c],
@@ -382,7 +383,7 @@
             if loading:
                 load_h(e).wait()
             mine = pl.ds(pl.multiple_of(e * slots, slots), slots)
-            for half in (0, 1):
+            for half in BOTH:
                 out = dot(hb[e], wdb[step % 2, :, half * HALF : (half + 1) * HALF]).astype(BF16)
                 for dx in range(side):
                     for dy in range(side):
@@ -394,31 +395,31 @@
         lax.fori_loop(0, experts, expert, 0)
 
     def send_rows(c):
-        for half in (0, 1):
+        for half in BOTH:
             for kind in (0, 1, 2, 3):
                 send(kind, half, c).start()
 
     def pass_rows(c):
         par = c % 3
-        for half in (0, 1):
+        for half in BOTH:
 
             @pl.when(c > 0)
             def _():
                 for kind in (4, 5):
                     send(kind, half, c - 1).wait_send()
 
-            for way in (0, 1):
+            for way in BOTH:
                 send(way, half, c).wait_recv()
                 for n in range(2):
                     r = 2 * way + n
                     total = dot(cm[half, 2, r], ob[half, par, 3 if way == 0 else 1, r])
                     tokb[half, way, n] = (total + dot(cm[half, 3, r], tran[half, c, way, n])).astype(BF16)
-            for way in (0, 1):
+            for way in BOTH:
                 send(way + 4, half, c).start()
 
     def relay(c):
         par = c % 3
-        for half in (0, 1):
+        for half in BOTH:
             for kind in (2, 3, 4, 5):
                 send(kind, half, c).wait_recv()
 
@@ -443,7 +444,7 @@
             yacc[:, at] += total(0)
 
     def near(c):
-        for half in (0, 1):
+        for half in BOTH:
 
             @pl.when(c > 0)
             def _():
@@ -460,7 +461,7 @@
             send(9, half, c).start()
 
     def finish(c):
-        for half in (0, 1):
+        for half in BOTH:
             for kind in (8, 9):
                 send(kind, half, c).wait_recv()
             at = pl.ds(pl.multiple_of(c * wide + half * HALF, HALF), HALF)
@@ -525,7 +526,7 @@
     send_rows(1)
 
     def select(some):
-        for half in (0, 1):
+        for half in BOTH:
             for i in some:
                 for r in range(side):
                     (g, at), device = pairs(place, half, i, r)
@@ -551,7 +552,7 @@
 
         @pl.when(c + 3 < chunks)
         def _():
-            for half in (0, 1):
+            for half in BOTH:
                 for kind in (0, 1, 2, 3):
                     send(kind, half, c).wait_send()
             down(c + 3)
@@ -572,7 +573,7 @@
 
     lax.fori_loop(0, chunks, end, 0)
 
-    for half in (0, 1):
+    for half in BOTH:
         for kind in (4, 5, 6, 7, 8, 9):
             send(kind, half, chunks - 1).wait_send()
         for c in (chunks - 3, chunks - 2, chunks - 1):

time: 234 us -> 234 us (level)
  no operation moved by 1% of the time
where the time goes in v4:
time: 234 us
  Pallas kernels  229 us (98%)
  local copies, waits for them, and re-layouts  2.46 us (1%)
    pallas_call x1, Pallas kernels, local(): pl.pallas_call(functools.partial(expert_in, side, slots, chunks), out_sha...  126 us
    pallas_call x1, Pallas kernels, local(): pl.pallas_call(functools.partial(expert_out, side, slots, chunks), out_sh...  103 us

profile of v4, /device:TPU:96, one launch (start us, length us, event | category | flops | bytes accessed | tf_op | source)
XLA Modules:
  0.0 233.6 jit_solution(1899553269558443165)
XLA Ops:
  0.0 0.7 convert_bitcast_fusion.1
  0.7 0.7 convert_bitcast_fusion
  1.4 0.6 pad_maximum_fusion.rt_ref
  2.0 125.9 %expert_in.1 = (bf16[5,512,1536]{2,1,0:T(8,128)(2,1)}, f32[2,2,4,16,256]{4,3,2,1,0:T(8,128)}) custom-call(f32[16,256]{1,0:T(8,128)} %pad_maximum_fusion.rt_ref, bf16[256,2560]{1,0:T(8,128)(2,1)} %bitcast.12, bf16[5,2560,1536]{2,1,0:T(8,128)(2,1)} %wg_hbm.1, bf16[5,2560,1536]{2,1,0:T(8,128)(2,1)} %wu_hbm.1), custom_call_target="tpu_custom_call" | custom-call | tf_op jit(solution)/shard_map/expert_in/pallas_call | solution.py:605
  128.0 103.2 %expert_out.1 = bf16[256,2560]{1,0:T(8,128)(2,1)} custom-call(f32[2,2,4,16,256]{4,3,2,1,0:T(8,128)} %get-tuple-element.7.rt_ref, bf16[256,2560]{1,0:T(8,128)(2,1)} %bitcast.13, bf16[5,512,1536]{2,1,0:T(8,128)(2,1)} %get-tuple-element.8.h_hbm, bf16[5,1536,2560]{2,1,0:T(8,128)(2,1)} %wd_hbm.1, bf16[2560,1536]{1,0:T(8,128)(2,1)} %sg_hbm.1, ...), custom_call_target="tpu_custom_call" | custom-call | tf_op jit(solution)/shard_map/expert_out/pallas_call | solution.py:639
  231.2 2.5 %copy.12 = bf16[1,1,256,2560]{3,2,1,0:T(8,128)(2,1)} copy(bf16[1,1,256,2560]{3,2,1,0:T(8,128)(2,1)} %bitcast.11) | data formatting | bytes 2621440
